TPU v7x, 32 devices: a whole 2x2x4 slice. The times are simulated.
32 devices in a mesh: head: 4 (over z), seq: 8 (over y, x, core).
Axes of the slice: x: 2, y: 2, z: 4, core: 2. Of those that a mesh axis runs over, the one named last changes fastest.
Arguments:
- queries: bfloat16 [1024, 8192], P('seq', 'head'), may hold values from -100 to 100
- keys: bfloat16 [1024, 1024], P('seq', 'head'), may hold values from -5 to 5
- values: bfloat16 [1024, 1024], P('seq', 'head'), may hold values from -6 to 6
- q_tangent: bfloat16 [1024, 8192], P('seq', 'head'), may hold values from -6 to 6
- k_tangent: bfloat16 [1024, 1024], P('seq', 'head'), may hold values from -6 to 6
- v_tangent: bfloat16 [1024, 1024], P('seq', 'head'), may hold values from -6 to 6
- out_grad: bfloat16 [1024, 8192], P('seq', 'head'), may hold values from -6 to 6
- block_order: int32 [8], replicated, may hold values from 0 to 7, each once
Outputs:
- dq_tangent: bfloat16 [1024, 8192], P('seq', 'head')
- dk_tangent: bfloat16 [1024, 1024], P('seq', 'head')
- dv_tangent: bfloat16 [1024, 1024], P('seq', 'head')
- squared_norm: float32 [], replicated
Inputs may be any that keep to these rules, and one draw needn't show every extreme that they name: `block_order`: every value of 0 to 7 appears once.
All inputs are finite; a program needn't handle non-finite values.
Results may differ from a plain program's by a relative error of at most 0.025.
Values may be sent and summed in bfloat16 or wider, within the bound.
No kernel may reach another device: no remote copies, remote signals or barrier semaphores. Data moves between devices by JAX's collectives and lax.ppermute only.
A program may use at most 64 MiB of HBM per device.

v0:
```python
import jax
import jax.numpy as jnp
from jax import lax
from jax.sharding import PartitionSpec as P

HD = 128
G = 8
neg_fill = -1e30


def body(queries, keys, values, q_tangent, k_tangent, v_tangent, out_grad, block_order):
    tokens = queries.shape[0]
    heads = keys.shape[1] // HD
    scaling = HD ** (-0.5)
    shards = lax.axis_size("seq")
    my_index = lax.axis_index("seq")
    my_block = block_order[my_index]
    query_pos = my_block * tokens + jnp.arange(tokens, dtype=jnp.int32)
    query_rows = queries.reshape(tokens, heads, G, HD)
    query_tan = q_tangent.reshape(tokens, heads, G, HD)
    grad_rows = out_grad.reshape(tokens, heads, G, HD)

    def block_scores(blocks, key_pos):
        key_blk, val_blk, key_tan, val_tan = [b.reshape(b.shape[0], heads, HD) for b in blocks]
        visible = (key_pos[None, :] <= query_pos[:, None])[None, None]
        s_main = (
            jnp.einsum("thgd,shd->hgts", query_rows, key_blk, preferred_element_type=jnp.float32)
            * scaling
        )
        s_tan = (
            jnp.einsum("thgd,shd->hgts", query_tan, key_blk, preferred_element_type=jnp.float32)
            + jnp.einsum("thgd,shd->hgts", query_rows, key_tan, preferred_element_type=jnp.float32)
        ) * scaling
        d_prob = jnp.einsum(
            "thgd,shd->hgts", grad_rows, val_blk, preferred_element_type=jnp.float32
        )
        d_prob_tan = jnp.einsum(
            "thgd,shd->hgts", grad_rows, val_tan, preferred_element_type=jnp.float32
        )
        return (visible, s_main, s_tan, d_prob, d_prob_tan, key_blk, key_tan)

    def add_stats(row_stats, blocks, key_pos):
        visible, s_main, s_tan, d_prob, d_prob_tan, key_blk, key_tan = block_scores(blocks, key_pos)
        row_max, row_total, tan_sum, grad_sum, cross_sum, extra_sum = row_stats
        new_max = jnp.maximum(row_max, jnp.max(jnp.where(visible, s_main, neg_fill), axis=-1))
        decay = jnp.exp(row_max - new_max)
        expo = jnp.where(visible, jnp.exp(s_main - new_max[..., None]), 0.0)
        return (
            new_max,
            row_total * decay + jnp.sum(expo, axis=-1),
            tan_sum * decay + jnp.sum(expo * s_tan, axis=-1),
            grad_sum * decay + jnp.sum(expo * d_prob, axis=-1),
            cross_sum * decay + jnp.sum(expo * s_tan * d_prob, axis=-1),
            extra_sum * decay + jnp.sum(expo * d_prob_tan, axis=-1),
        )

    def block_grads(finished, blocks, key_pos):
        visible, s_main, s_tan, d_prob, d_prob_tan, key_blk, key_tan = block_scores(blocks, key_pos)
        row_max, row_total, tan_mean, delta, delta_tan = [f[..., None] for f in finished]
        prob = jnp.where(visible, jnp.exp(s_main - row_max), 0.0) / row_total
        prob_tan = prob * (s_tan - tan_mean)
        d_score = prob * (d_prob - delta)
        d_score_tan = prob_tan * (d_prob - delta) + prob * (d_prob_tan - delta_tan)
        prob_tan_b = prob_tan.astype(jnp.bfloat16)
        d_score_b = d_score.astype(jnp.bfloat16)
        d_score_tan_b = d_score_tan.astype(jnp.bfloat16)
        dq_part = (
            jnp.einsum("hgts,shd->thgd", d_score_tan_b, key_blk, preferred_element_type=jnp.float32)
            + jnp.einsum("hgts,shd->thgd", d_score_b, key_tan, preferred_element_type=jnp.float32)
        ) * scaling
        dk_part = (
            jnp.einsum(
                "hgts,thgd->shd", d_score_tan_b, query_rows, preferred_element_type=jnp.float32
            )
            + jnp.einsum("hgts,thgd->shd", d_score_b, query_tan, preferred_element_type=jnp.float32)
        ) * scaling
        dv_part = jnp.einsum(
            "hgts,thgd->shd", prob_tan_b, grad_rows, preferred_element_type=jnp.float32
        )
        key_rows = key_pos.shape[0]
        return (
            dq_part,
            dk_part.reshape(key_rows, heads * HD),
            dv_part.reshape(key_rows, heads * HD),
        )

    row_zero = jnp.zeros((heads, G, tokens), jnp.float32)
    start_stats = (
        jnp.full((heads, G, tokens), neg_fill, jnp.float32),
        row_zero,
        row_zero,
        row_zero,
        row_zero,
        row_zero,
    )
    dq_zero = jnp.zeros((tokens, heads, G, HD), jnp.float32)
    whole = (
        lax.all_gather(keys, "seq", axis=0, tiled=True),
        lax.all_gather(values, "seq", axis=0, tiled=True),
        lax.all_gather(k_tangent, "seq", axis=0, tiled=True),
        lax.all_gather(v_tangent, "seq", axis=0, tiled=True),
    )
    inverse = (
        jnp.zeros((shards,), jnp.int32).at[block_order].set(jnp.arange(shards, dtype=jnp.int32))
    )
    all_rows = shards * tokens
    ordered = tuple((w.reshape(shards, tokens, -1)[inverse].reshape(all_rows, -1) for w in whole))
    block_rows = min(512, all_rows)
    visits = (my_block * tokens + tokens + block_rows - 1) // block_rows

    def slice_blocks(block_index):
        offset = block_index * block_rows
        pieces = tuple((lax.dynamic_slice_in_dim(o, offset, block_rows, 0) for o in ordered))
        return (pieces, offset + jnp.arange(block_rows, dtype=jnp.int32))

    def stats_turn(block_index, row_stats):
        pieces, key_pos = slice_blocks(block_index)
        return add_stats(row_stats, pieces, key_pos)

    row_max, row_total, tan_sum, grad_sum, cross_sum, extra_sum = lax.fori_loop(
        0, visits, stats_turn, start_stats
    )
    tan_mean = tan_sum / row_total
    delta = grad_sum / row_total
    delta_tan = cross_sum / row_total - tan_mean * delta + extra_sum / row_total
    finished = (row_max, row_total, tan_mean, delta, delta_tan)

    def grad_turn(block_index, carry):
        dq_acc, dk_sorted, dv_sorted = carry
        pieces, key_pos = slice_blocks(block_index)
        dq_part, dk_part, dv_part = block_grads(finished, pieces, key_pos)
        offset = block_index * block_rows
        return (
            dq_acc + dq_part,
            lax.dynamic_update_slice_in_dim(dk_sorted, dk_part, offset, 0),
            lax.dynamic_update_slice_in_dim(dv_sorted, dv_part, offset, 0),
        )

    side_zero = jnp.zeros((all_rows, heads * HD), jnp.float32)
    dq_acc, dk_sorted, dv_sorted = lax.fori_loop(
        0, visits, grad_turn, (dq_zero, side_zero, side_zero)
    )
    dk_local = dk_sorted.reshape(shards, tokens, -1)[block_order].reshape(all_rows, -1)
    dv_local = dv_sorted.reshape(shards, tokens, -1)[block_order].reshape(all_rows, -1)
    dk_total, dv_total = (
        lax.psum_scatter(
            dk_local.astype(jnp.bfloat16), "seq", scatter_dimension=0, tiled=True
        ).astype(jnp.float32),
        lax.psum_scatter(
            dv_local.astype(jnp.bfloat16), "seq", scatter_dimension=0, tiled=True
        ).astype(jnp.float32),
    )
    dq_out = dq_acc.reshape(tokens, heads * G * HD).astype(jnp.bfloat16)
    dk_out = dk_total.astype(jnp.bfloat16)
    dv_out = dv_total.astype(jnp.bfloat16)
    dq_wide = dq_out.astype(jnp.float32)
    dk_wide = dk_out.astype(jnp.float32)
    dv_wide = dv_out.astype(jnp.float32)
    local_term = (
        jnp.sum(dq_wide * dq_wide) + jnp.sum(dk_wide * dk_wide) + jnp.sum(dv_wide * dv_wide)
    )
    squared_norm = lax.psum(local_term, ("head", "seq"))
    return (dq_out, dk_out, dv_out, squared_norm)


def solution(mesh):
    placed = (
        P("seq", "head"),
        P("seq", "head"),
        P("seq", "head"),
        P("seq", "head"),
        P("seq", "head"),
        P("seq", "head"),
        P("seq", "head"),
        P(),
    )
    return jax.shard_map(
        body,
        mesh=mesh,
        in_specs=placed,
        out_specs=(P("seq", "head"), P("seq", "head"), P("seq", "head"), P()),
        check_vma=False,
    )
```

profile of v0, /device:TPU:0, one launch (start us, length us, event | category | flops | bytes accessed | tf_op | source)
XLA Modules:
  0.0 250.2 jit_solution(16309284983064121922)
XLA Ops:
  7.2 0.0 reduce-scatter.3.cloned.1.call-start
  7.2 1.2 dynamic_slice.27
  9.1 0.7 compare_select_fusion.1
  9.8 0.6 pad_clamp_fusion
  10.4 0.6 scatter_custom_fusion
  11.0 11.6 %all_gather.13 = bf16[1024,256]{1,0:T(8,128)(2,1)S(1)} all-gather(bf16[128,256]{1,0:T(8,128)(2,1)} %param.16), channel_id=1, replica_groups=mesh['head'=4,'seq'=8] {'seq'}, dimensions={0}, use_global_device_ids=true | all-gather | bytes 589824 | tf_op jit(solution)/shard_map/all_gather | solution.py:100
  22.7 0.6 gather_fusion.1
  23.2 0.2 copy.86
  23.5 9.7 %all_gather.14 = bf16[1024,256]{1,0:T(8,128)(2,1)S(1)} all-gather(bf16[128,256]{1,0:T(8,128)(2,1)} %param.14), channel_id=1, replica_groups=mesh['head'=4,'seq'=8] {'seq'}, dimensions={0}, use_global_device_ids=true | all-gather | bytes 589824 | tf_op jit(solution)/shard_map/all_gather | solution.py:99
  33.1 0.6 gather_fusion.2
  33.7 1.0 copy.87
  34.8 9.2 %all_gather.15 = bf16[1024,256]{1,0:T(8,128)(2,1)S(1)} all-gather(bf16[128,256]{1,0:T(8,128)(2,1)S(1)} %copy-done.16), channel_id=1, replica_groups=mesh['head'=4,'seq'=8] {'seq'}, dimensions={0}, use_global_device_ids=true | all-gather | bytes 589824 | tf_op jit(solution)/shard_map/all_gather | solution.py:101
  43.9 0.6 gather_fusion.3
  44.5 1.1 copy.89
  45.6 9.5 %all_gather.12 = bf16[1024,256]{1,0:T(8,128)(2,1)S(1)} all-gather(bf16[128,256]{1,0:T(8,128)(2,1)S(1)} %copy-done.17), channel_id=1, replica_groups=mesh['head'=4,'seq'=8] {'seq'}, dimensions={0}, use_global_device_ids=true | all-gather | bytes 589824 | tf_op jit(solution)/shard_map/all_gather | solution.py:98
  55.1 0.6 gather_fusion
  55.7 1.0 copy.90
  56.7 0.3 copy.80
  56.9 0.3 copy.84
  57.2 0.3 copy.81
  57.5 0.3 copy.85
  57.8 1.3 copy.82
  59.1 1.0 copy.88
  60.2 7.8 %while.36 = (s32[]{:T(128)}, f32[2,8,128]{2,1,0:T(8,128)S(1)}, f32[2,8,128]{2,1,0:T(8,128)S(1)}, f32[2,8,128]{2,1,0:T(8,128)S(1)}, f32[2,8,128]{2,1,0:T(8,128)S(...) while((s32[]{:T(128)}, f32[2,8,128]{2,1,0:T(8,128)S(1)}, ...), condition=%wide.region_8.9_spmd.clone, body=%wide.region_1.8_spmd.clone.sunk | while | flops 1366372992 | bytes 46478664 | solution.py:120
  60.2 1.0 constant_dynamic-slice_fusion.14
  61.2 0.1 broadcast_compare_fusion.4
  61.4 0.8 fusion.112
  62.2 0.8 fusion.113
  63.0 1.5 bitcast_multiply_fusion.5
  64.6 2.1 fusion.114
  66.6 1.3 fusion.115
  68.0 1.1 broadcast_in_dim.61
  69.1 0.8 broadcast_in_dim.62.clone
  70.0 0.8 broadcast_in_dim.62.clone2
  70.8 23.7 %while.37 = (s32[]{:T(128)}, f32[128,2,8,128]{0,3,2,1:T(8,128)}, bf16[1024,256]{1,0:T(8,128)(2,1)}, bf16[1024,256]{1,0:T(8,128)(2,1)}, s32[]{:T(128)}, /*index=5...) while((s32[]{:T(128)}, f32[128,2,8,128]{0,3,2,1:T(8,128)}, ...), condition=%wide.region_10.11_spmd.clone, body=%wide.region_9.10_spmd.clone.sunk | while | flops 2704474624 | bytes 123131472 | solution.py:140
  70.8 1.2 constant_dynamic-slice_fusion.17
  72.0 0.7 fusion.136
  72.8 0.1 broadcast_compare_fusion.5
  73.0 1.7 multiply_convert_fusion.2
  74.7 0.7 fusion.137
  75.5 1.0 fusion.138
  76.5 0.1 copy-done.11
  76.6 1.4 fusion.139
  78.1 0.4 copy-done
  78.4 1.8 convolution_bitcast_fusion.3
  80.3 1.5 fusion.143
  81.8 1.8 copy.153
  83.6 3.7 %fusion.142 = bf16[2,512,128,1]{1,2,3,0:T(8,128)(2,1)} fusion(bf16[128,2,8,128]{0,3,2,1:T(8,128)(2,1)S(1)} %get-tuple-element.796, f32[2,8,128,512]{2,3,1,0:T(8,128)} %copy-done), kind=kOutput, calls=%fused_computation.47.clone.1 | convolution fusion | flops 269484032 | bytes 4980736 | tf_op jit(solution)/shard_map/while/body/hgts,thgd->shd/dot_general | solution.py:77
  87.3 1.8 copy.152
  89.1 2.0 constant_dynamic-update-slice_fusion.3
  91.1 0.4 fusion.140
  91.6 2.9 %fusion.141 = f32[128,2,8,128]{0,3,2,1:T(8,128)} fusion(f32[128,2,8,128]{0,3,2,1:T(8,128)} %get-tuple-element.762, f32[2,128,8,128]{3,1,2,0:T(8,128)S(1)} %fusion.140, bf16[512,2,128,1]{0,2,3,1:T(8,128)(2,1)S(1)} %bitcast.291, bf16[2,8,128,512]{2,3,1,0:T(8,128)(2,1)S(1)} %copy-done.2), kind=kOutput, calls=%fused_computation.52.clone.1 | convolution fusion | flops 269221888 | bytes 5505024 | tf_op jit(solution)/shard_map/while/body/hgts,shd->thgd/dot_general | solution.py:69
  94.5 2.5 %gather_fusion.4 = bf16[8,128,256]{2,1,0:T(8,128)(2,1)} fusion(bf16[8,128,256]{2,1,0:T(8,128)(2,1)} %bitcast.302, s32[1024]{0:T(1024)} %pad_clamp_fusion), kind=kCustom, calls=%fused_computation.4 | custom fusion | bytes 1048608 | tf_op jit(solution)/shard_map/gather | solution.py:143
  97.0 0.0 reduce-scatter.3.cloned.1.call-update
  97.1 0.0 reduce-scatter.5.cloned.1.call-start
  97.1 2.5 %gather_fusion.5 = bf16[8,128,256]{2,1,0:T(8,128)(2,1)} fusion(bf16[8,128,256]{2,1,0:T(8,128)(2,1)} %bitcast.303, s32[1024]{0:T(1024)} %pad_clamp_fusion), kind=kCustom, calls=%fused_computation.5 | custom fusion | bytes 1048608 | tf_op jit(solution)/shard_map/gather | solution.py:144
  99.6 0.0 reduce-scatter.5.cloned.1.call-update
  99.7 2.1 multiply_reduce_fusion
  101.8 61.4 %reduce-scatter.3.cloned.1.call-done = bf16[128,256]{1,0:T(8,128)(2,1)} async-done(((bf16[1024,256]{1,0:T(8,128)(2,1)}), bf16[128,256]{1,0:T(8,128)(2,1)}) %reduce-scatter.3.cloned.1.call-update) | async-done | bytes 65552 | tf_op jit(solution)/shard_map/reduce_scatter | solution.py:146
  163.2 1.6 multiply_reduce_fusion.2
  166.1 34.9 %reduce-scatter.5.cloned.1.call-done = bf16[128,256]{1,0:T(8,128)(2,1)} async-done(((bf16[1024,256]{1,0:T(8,128)(2,1)}), bf16[128,256]{1,0:T(8,128)(2,1)}) %reduce-scatter.5.cloned.1.call-update) | async-done | bytes 65552 | tf_op jit(solution)/shard_map/reduce_scatter | solution.py:149
  201.0 1.5 multiply_reduce_fusion.1
  203.2 1.0 copy.122
  204.2 39.2 %psum.7 = f32[]{:T(128)} all-reduce(f32[]{:T(128)S(6)} %add.127), channel_id=1, replica_groups=mesh['head'=4,'seq'=8] {'head','seq'}, use_global_device_ids=true, to_apply=%region_16.17 | all-reduce | flops 1 | bytes 8 | tf_op jit(solution)/shard_map/psum | solution.py:162
  (56 shorter events, 0.3 us)
Async XLA Ops:
  7.2 27.6 %copy-start.16 = (bf16[128,256]{1,0:T(8,128)(2,1)S(1)}, bf16[128,256]{1,0:T(8,128)(2,1)}, u32[]{:S(2)}) copy-start(bf16[128,256]{1,0:T(8,128)(2,1)} %param.17) | copy-start | bytes 196612
  7.2 38.4 %copy-start.17 = (bf16[128,256]{1,0:T(8,128)(2,1)S(1)}, bf16[128,256]{1,0:T(8,128)(2,1)}, u32[]{:S(2)}) copy-start(bf16[128,256]{1,0:T(8,128)(2,1)} %param.13) | copy-start | bytes 196612
  7.2 156.0 %reduce-scatter.3.cloned.1.call-start = ((), (), s32[]{:S(2)}) async-start(), calls=%async_computation.2 | async-start | bytes 589824 | tf_op jit(solution)/shard_map/reduce_scatter | solution.py:146
  23.5 33.2 %copy-start.13 = (bf16[128,2048]{1,0:T(8,128)(2,1)S(1)}, bf16[128,2048]{1,0:T(8,128)(2,1)}, u32[]{:S(2)}) copy-start(bf16[128,2048]{1,0:T(8,128)(2,1)} %param.12) | copy-start | bytes 1572868
  33.7 23.5 %copy-start.14 = (bf16[128,2048]{1,0:T(8,128)(2,1)S(1)}, bf16[128,2048]{1,0:T(8,128)(2,1)}, u32[]{:S(2)}) copy-start(bf16[128,2048]{1,0:T(8,128)(2,1)} %param.15) | copy-start | bytes 1572868
  63.0 1.5 copy-start.9
  63.0 1.5 copy-start.10
  63.0 1.6 copy-start.15
  70.8 3.9 %copy-start.3 = (bf16[128,2,8,128]{0,3,2,1:T(8,128)(2,1)}, bf16[128,2,8,128]{0,3,2,1:T(8,128)(2,1)S(1)}, u32[]{:S(2)}) copy-start(bf16[128,2,8,128]{0,3,2,1:T(8,128)(2,1)S(1)} %get-tuple-element.792) | copy-start | bytes 1572868 | tf_op jit(solution)/shard_map/while
  70.8 4.6 %copy-start.7 = (bf16[1024,256]{0,1:T(8,128)(2,1)}, bf16[1024,256]{0,1:T(8,128)(2,1)S(1)}, u32[]{:S(2)}) copy-start(bf16[1024,256]{0,1:T(8,128)(2,1)S(1)} %get-tuple-element.793) | copy-start | bytes 1572868 | tf_op jit(solution)/shard_map/while
  70.8 2.0 copy-start.12
  74.7 3.8 %copy-start.1 = (bf16[2,8,128,512]{2,3,1,0:T(8,128)(2,1)}, bf16[2,8,128,512]{2,3,1,0:T(8,128)(2,1)S(1)}, u32[]{:S(2)}) copy-start(bf16[2,8,128,512]{2,3,1,0:T(8,128)(2,1)S(1)} %get-tuple-element.676) | copy-start | bytes 6291460 | tf_op jit(solution)/shard_map/while
  75.5 1.0 copy-start.5
  75.5 1.1 copy-start.11
  76.5 1.9 copy-start
  89.1 2.5 copy-start.2
  89.1 2.5 copy-start.6
  91.6 2.9 %copy-start.4 = (bf16[128,2,8,128]{0,3,2,1:T(8,128)(2,1)S(1)}, bf16[128,2,8,128]{0,3,2,1:T(8,128)(2,1)}, u32[]{:S(2)}) copy-start(bf16[128,2,8,128]{0,3,2,1:T(8,128)(2,1)} %copy-done.3) | copy-start | bytes 1572868 | tf_op jit(solution)/shard_map/while
  91.6 2.9 %copy-start.8 = (bf16[1024,256]{0,1:T(8,128)(2,1)S(1)}, bf16[1024,256]{0,1:T(8,128)(2,1)}, u32[]{:S(2)}) copy-start(bf16[1024,256]{0,1:T(8,128)(2,1)} %copy-done.7) | copy-start | bytes 1572868 | tf_op jit(solution)/shard_map/while
  97.1 104.0 %reduce-scatter.5.cloned.1.call-start = ((), (), s32[]{:S(2)}) async-start(), calls=%async_computation.3 | async-start | bytes 589824 | tf_op jit(solution)/shard_map/reduce_scatter | solution.py:149
Sparse Core Ops, SparseCore 0:
  97.2 65.9 reduce-scatter.2
  166.9 34.1 reduce-scatter.4
where the time goes:
time: 251 us; the launch traced here: 250 us
  waiting for transfers between devices  96.4 us (38%)
  blocking collectives  79.2 us (32%)
  local copies, waits for them, and re-layouts  28.2 us (11%)
  matrix products  22.4 us (9%)
  between operations  16.9 us (7%)
  other arithmetic  6.74 us (3%)
    reduce_scatter x1, waiting for transfers between devices, body(): lax.psum_scatter(dk_local.astype(jnp.bfloat16), 'seq', scatter_dimension=...  61.4 us
    psum x1, blocking collectives, body(): squared_norm = lax.psum(local_term, ('head', 'seq'))  39.2 us
    reduce_scatter x1, waiting for transfers between devices, body(): lax.psum_scatter(dv_local.astype(jnp.bfloat16), 'seq', scatter_dimension=...  34.9 us
    all_gather x1, blocking collectives, body(): lax.all_gather(k_tangent, 'seq', axis=0, tiled=True)  11.6 us
    all_gather x1, blocking collectives, body(): lax.all_gather(values, 'seq', axis=0, tiled=True)  9.67 us
    all_gather x1, blocking collectives, body(): lax.all_gather(keys, 'seq', axis=0, tiled=True)  9.5 us
    all_gather x1, blocking collectives, body(): lax.all_gather(v_tangent, 'seq', axis=0, tiled=True)  9.17 us
    unnamed x18, local copies, waits for them, and re-layouts  6.73 us
  transfers between devices with their start and end apart: 2, of which 2 were waited for; matrix products, arithmetic and copies ran while one was open for 2% of the time, Pallas kernels for 0%

commit v1 on v0

--- a/solution.py
+++ b/solution.py
@@ -159,7 +159,7 @@
     local_term = (
         jnp.sum(dq_wide * dq_wide) + jnp.sum(dk_wide * dk_wide) + jnp.sum(dv_wide * dv_wide)
     )
-    squared_norm = lax.psum(local_term, ("head", "seq"))
+    squared_norm = lax.psum(lax.psum(local_term, "seq"), "head")
     return (dq_out, dk_out, dv_out, squared_norm)
 
 

time: 251 us -> 237 us (0.944)
  blocking collectives: 79.2 us -> 64.9 us
    psum x1 -> x2, blocking collectives: 39.2 us -> 24.9 us  [body(): squared_norm = lax.psum(lax.psum(local_term, 'seq'), 'head')]
  transfers between devices with their start and end apart: 2 -> 2, of which waited for: 2 -> 2; matrix products, arithmetic and copies ran while one was open for 2% -> 3% of each run, Pallas kernels for 0% -> 0%
where the time goes in v1:
time: 237 us; the launch traced here: 236 us
  waiting for transfers between devices  96.4 us (41%)
  blocking collectives  64.9 us (27%)
  local copies, waits for them, and re-layouts  28.2 us (12%)
  matrix products  22.4 us (9%)
  between operations  16.9 us (7%)
  other arithmetic  6.74 us (3%)
    reduce_scatter x1, waiting for transfers between devices, body(): lax.psum_scatter(dk_local.astype(jnp.bfloat16), 'seq', scatter_dimension=...  61.4 us
    reduce_scatter x1, waiting for transfers between devices, body(): lax.psum_scatter(dv_local.astype(jnp.bfloat16), 'seq', scatter_dimension=...  34.9 us
    psum x2, blocking collectives, body(): squared_norm = lax.psum(lax.psum(local_term, 'seq'), 'head')  24.9 us
    all_gather x1, blocking collectives, body(): lax.all_gather(k_tangent, 'seq', axis=0, tiled=True)  11.6 us
    all_gather x1, blocking collectives, body(): lax.all_gather(values, 'seq', axis=0, tiled=True)  9.67 us
    all_gather x1, blocking collectives, body(): lax.all_gather(keys, 'seq', axis=0, tiled=True)  9.5 us
    all_gather x1, blocking collectives, body(): lax.all_gather(v_tangent, 'seq', axis=0, tiled=True)  9.17 us
    unnamed x18, local copies, waits for them, and re-layouts  6.73 us
  transfers between devices with their start and end apart: 2, of which 2 were waited for; matrix products, arithmetic and copies ran while one was open for 3% of the time, Pallas kernels for 0%

profile of v1, /device:TPU:0, one launch (start us, length us, event | category | flops | bytes accessed | tf_op | source)
XLA Modules:
  0.0 235.9 jit_solution(6617886108475450314)
XLA Ops:
  7.2 0.0 reduce-scatter.3.cloned.1.call-start
  7.2 1.2 dynamic_slice.27
  9.1 0.7 compare_select_fusion.1
  9.8 0.6 pad_clamp_fusion
  10.4 0.6 scatter_custom_fusion
  11.0 11.6 %all_gather.13 = bf16[1024,256]{1,0:T(8,128)(2,1)S(1)} all-gather(bf16[128,256]{1,0:T(8,128)(2,1)} %param.16), channel_id=1, replica_groups=mesh['head'=4,'seq'=8] {'seq'}, dimensions={0}, use_global_device_ids=true | all-gather | bytes 589824 | tf_op jit(solution)/shard_map/all_gather | solution.py:100
  22.7 0.6 gather_fusion.1
  23.2 0.2 copy.86
  23.5 9.7 %all_gather.14 = bf16[1024,256]{1,0:T(8,128)(2,1)S(1)} all-gather(bf16[128,256]{1,0:T(8,128)(2,1)} %param.14), channel_id=1, replica_groups=mesh['head'=4,'seq'=8] {'seq'}, dimensions={0}, use_global_device_ids=true | all-gather | bytes 589824 | tf_op jit(solution)/shard_map/all_gather | solution.py:99
  33.1 0.6 gather_fusion.2
  33.7 1.0 copy.87
  34.8 9.2 %all_gather.15 = bf16[1024,256]{1,0:T(8,128)(2,1)S(1)} all-gather(bf16[128,256]{1,0:T(8,128)(2,1)S(1)} %copy-done.16), channel_id=1, replica_groups=mesh['head'=4,'seq'=8] {'seq'}, dimensions={0}, use_global_device_ids=true | all-gather | bytes 589824 | tf_op jit(solution)/shard_map/all_gather | solution.py:101
  43.9 0.6 gather_fusion.3
  44.5 1.1 copy.89
  45.6 9.5 %all_gather.12 = bf16[1024,256]{1,0:T(8,128)(2,1)S(1)} all-gather(bf16[128,256]{1,0:T(8,128)(2,1)S(1)} %copy-done.17), channel_id=1, replica_groups=mesh['head'=4,'seq'=8] {'seq'}, dimensions={0}, use_global_device_ids=true | all-gather | bytes 589824 | tf_op jit(solution)/shard_map/all_gather | solution.py:98
  55.1 0.6 gather_fusion
  55.7 1.0 copy.90
  56.7 0.3 copy.80
  56.9 0.3 copy.84
  57.2 0.3 copy.81
  57.5 0.3 copy.85
  57.8 1.3 copy.82
  59.1 1.0 copy.88
  60.2 7.8 %while.36 = (s32[]{:T(128)}, f32[2,8,128]{2,1,0:T(8,128)S(1)}, f32[2,8,128]{2,1,0:T(8,128)S(1)}, f32[2,8,128]{2,1,0:T(8,128)S(1)}, f32[2,8,128]{2,1,0:T(8,128)S(...) while((s32[]{:T(128)}, f32[2,8,128]{2,1,0:T(8,128)S(1)}, ...), condition=%wide.region_8.9_spmd.clone, body=%wide.region_1.8_spmd.clone.sunk | while | flops 1366372992 | bytes 46478664 | solution.py:120
  60.2 1.0 constant_dynamic-slice_fusion.14
  61.2 0.1 broadcast_compare_fusion.4
  61.4 0.8 fusion.112
  62.2 0.8 fusion.113
  63.0 1.5 bitcast_multiply_fusion.5
  64.6 2.1 fusion.114
  66.6 1.3 fusion.115
  68.0 1.1 broadcast_in_dim.61
  69.1 0.8 broadcast_in_dim.62.clone
  70.0 0.8 broadcast_in_dim.62.clone2
  70.8 23.7 %while.37 = (s32[]{:T(128)}, f32[128,2,8,128]{0,3,2,1:T(8,128)}, bf16[1024,256]{1,0:T(8,128)(2,1)}, bf16[1024,256]{1,0:T(8,128)(2,1)}, s32[]{:T(128)}, /*index=5...) while((s32[]{:T(128)}, f32[128,2,8,128]{0,3,2,1:T(8,128)}, ...), condition=%wide.region_10.11_spmd.clone, body=%wide.region_9.10_spmd.clone.sunk | while | flops 2704474624 | bytes 123131472 | solution.py:140
  70.8 1.2 constant_dynamic-slice_fusion.17
  72.0 0.7 fusion.136
  72.8 0.1 broadcast_compare_fusion.5
  73.0 1.7 multiply_convert_fusion.2
  74.7 0.7 fusion.137
  75.5 1.0 fusion.138
  76.5 0.1 copy-done.11
  76.6 1.4 fusion.139
  78.1 0.4 copy-done
  78.4 1.8 convolution_bitcast_fusion.3
  80.3 1.5 fusion.143
  81.8 1.8 copy.153
  83.6 3.7 %fusion.142 = bf16[2,512,128,1]{1,2,3,0:T(8,128)(2,1)} fusion(bf16[128,2,8,128]{0,3,2,1:T(8,128)(2,1)S(1)} %get-tuple-element.796, f32[2,8,128,512]{2,3,1,0:T(8,128)} %copy-done), kind=kOutput, calls=%fused_computation.47.clone.1 | convolution fusion | flops 269484032 | bytes 4980736 | tf_op jit(solution)/shard_map/while/body/hgts,thgd->shd/dot_general | solution.py:77
  87.3 1.8 copy.152
  89.1 2.0 constant_dynamic-update-slice_fusion.3
  91.1 0.4 fusion.140
  91.6 2.9 %fusion.141 = f32[128,2,8,128]{0,3,2,1:T(8,128)} fusion(f32[128,2,8,128]{0,3,2,1:T(8,128)} %get-tuple-element.762, f32[2,128,8,128]{3,1,2,0:T(8,128)S(1)} %fusion.140, bf16[512,2,128,1]{0,2,3,1:T(8,128)(2,1)S(1)} %bitcast.291, bf16[2,8,128,512]{2,3,1,0:T(8,128)(2,1)S(1)} %copy-done.2), kind=kOutput, calls=%fused_computation.52.clone.1 | convolution fusion | flops 269221888 | bytes 5505024 | tf_op jit(solution)/shard_map/while/body/hgts,shd->thgd/dot_general | solution.py:69
  94.5 2.5 %gather_fusion.4 = bf16[8,128,256]{2,1,0:T(8,128)(2,1)} fusion(bf16[8,128,256]{2,1,0:T(8,128)(2,1)} %bitcast.302, s32[1024]{0:T(1024)} %pad_clamp_fusion), kind=kCustom, calls=%fused_computation.4 | custom fusion | bytes 1048608 | tf_op jit(solution)/shard_map/gather | solution.py:143
  97.0 0.0 reduce-scatter.3.cloned.1.call-update
  97.1 0.0 reduce-scatter.5.cloned.1.call-start
  97.1 2.5 %gather_fusion.5 = bf16[8,128,256]{2,1,0:T(8,128)(2,1)} fusion(bf16[8,128,256]{2,1,0:T(8,128)(2,1)} %bitcast.303, s32[1024]{0:T(1024)} %pad_clamp_fusion), kind=kCustom, calls=%fused_computation.5 | custom fusion | bytes 1048608 | tf_op jit(solution)/shard_map/gather | solution.py:144
  99.7 2.1 multiply_reduce_fusion
  101.8 61.4 %reduce-scatter.3.cloned.1.call-done = bf16[128,256]{1,0:T(8,128)(2,1)} async-done(((bf16[1024,256]{1,0:T(8,128)(2,1)}), bf16[128,256]{1,0:T(8,128)(2,1)}) %reduce-scatter.3.cloned.1.call-update) | async-done | bytes 65552 | tf_op jit(solution)/shard_map/reduce_scatter | solution.py:146
  163.2 1.6 multiply_reduce_fusion.2
  166.1 34.9 %reduce-scatter.5.cloned.1.call-done = bf16[128,256]{1,0:T(8,128)(2,1)} async-done(((bf16[1024,256]{1,0:T(8,128)(2,1)}), bf16[128,256]{1,0:T(8,128)(2,1)}) %reduce-scatter.5.cloned.1.call-update) | async-done | bytes 65552 | tf_op jit(solution)/shard_map/reduce_scatter | solution.py:149
  201.0 1.5 multiply_reduce_fusion.1
  203.2 12.7 %psum.14 = f32[]{:T(128)} all-reduce(f32[]{:T(128)S(6)} %add.129), channel_id=1, replica_groups=mesh['head'=4,'seq'=8] {'seq'}, use_global_device_ids=true, to_apply=%region_16.17 | all-reduce | flops 1 | bytes 8 | tf_op jit(solution)/shard_map/psum | solution.py:162
  215.8 1.0 copy.122
  216.8 12.3 %psum.15 = f32[]{:T(128)} all-reduce(f32[]{:T(128)} %psum.14), channel_id=1, replica_groups=mesh['head'=4,'seq'=8] {'head'}, use_global_device_ids=true, to_apply=%region_17.18 | all-reduce | flops 1 | bytes 8 | tf_op jit(solution)/shard_map/psum | solution.py:162
  (57 shorter events, 0.3 us)
Async XLA Ops:
  7.2 27.6 %copy-start.16 = (bf16[128,256]{1,0:T(8,128)(2,1)S(1)}, bf16[128,256]{1,0:T(8,128)(2,1)}, u32[]{:S(2)}) copy-start(bf16[128,256]{1,0:T(8,128)(2,1)} %param.17) | copy-start | bytes 196612
  7.2 38.4 %copy-start.17 = (bf16[128,256]{1,0:T(8,128)(2,1)S(1)}, bf16[128,256]{1,0:T(8,128)(2,1)}, u32[]{:S(2)}) copy-start(bf16[128,256]{1,0:T(8,128)(2,1)} %param.13) | copy-start | bytes 196612
  7.2 156.0 %reduce-scatter.3.cloned.1.call-start = ((), (), s32[]{:S(2)}) async-start(), calls=%async_computation.2 | async-start | bytes 589824 | tf_op jit(solution)/shard_map/reduce_scatter | solution.py:146
  23.5 33.2 %copy-start.13 = (bf16[128,2048]{1,0:T(8,128)(2,1)S(1)}, bf16[128,2048]{1,0:T(8,128)(2,1)}, u32[]{:S(2)}) copy-start(bf16[128,2048]{1,0:T(8,128)(2,1)} %param.12) | copy-start | bytes 1572868
  33.7 23.5 %copy-start.14 = (bf16[128,2048]{1,0:T(8,128)(2,1)S(1)}, bf16[128,2048]{1,0:T(8,128)(2,1)}, u32[]{:S(2)}) copy-start(bf16[128,2048]{1,0:T(8,128)(2,1)} %param.15) | copy-start | bytes 1572868
  63.0 1.5 copy-start.9
  63.0 1.5 copy-start.10
  63.0 1.6 copy-start.15
  70.8 3.9 %copy-start.3 = (bf16[128,2,8,128]{0,3,2,1:T(8,128)(2,1)}, bf16[128,2,8,128]{0,3,2,1:T(8,128)(2,1)S(1)}, u32[]{:S(2)}) copy-start(bf16[128,2,8,128]{0,3,2,1:T(8,128)(2,1)S(1)} %get-tuple-element.792) | copy-start | bytes 1572868 | tf_op jit(solution)/shard_map/while
  70.8 4.6 %copy-start.7 = (bf16[1024,256]{0,1:T(8,128)(2,1)}, bf16[1024,256]{0,1:T(8,128)(2,1)S(1)}, u32[]{:S(2)}) copy-start(bf16[1024,256]{0,1:T(8,128)(2,1)S(1)} %get-tuple-element.793) | copy-start | bytes 1572868 | tf_op jit(solution)/shard_map/while
  70.8 2.0 copy-start.12
  74.7 3.8 %copy-start.1 = (bf16[2,8,128,512]{2,3,1,0:T(8,128)(2,1)}, bf16[2,8,128,512]{2,3,1,0:T(8,128)(2,1)S(1)}, u32[]{:S(2)}) copy-start(bf16[2,8,128,512]{2,3,1,0:T(8,128)(2,1)S(1)} %get-tuple-element.676) | copy-start | bytes 6291460 | tf_op jit(solution)/shard_map/while
  75.5 1.0 copy-start.5
  75.5 1.1 copy-start.11
  76.5 1.9 copy-start
  89.1 2.5 %copy-start.2 = (bf16[2,8,128,512]{2,3,1,0:T(8,128)(2,1)S(1)}, bf16[2,8,128,512]{2,3,1,0:T(8,128)(2,1)}, u32[]{:S(2)}) copy-start(bf16[2,8,128,512]{2,3,1,0:T(8,128)(2,1)} %copy-done.1) | copy-start | bytes 6291460 | tf_op jit(solution)/shard_map/while
  89.1 2.5 %copy-start.6 = (bf16[512,256]{0,1:T(8,128)(2,1)S(1)}, bf16[512,256]{0,1:T(8,128)(2,1)}, u32[]{:S(2)}) copy-start(bf16[512,256]{0,1:T(8,128)(2,1)} %copy-done.5) | copy-start | bytes 786436 | tf_op jit(solution)/shard_map/while
  91.6 2.9 %copy-start.4 = (bf16[128,2,8,128]{0,3,2,1:T(8,128)(2,1)S(1)}, bf16[128,2,8,128]{0,3,2,1:T(8,128)(2,1)}, u32[]{:S(2)}) copy-start(bf16[128,2,8,128]{0,3,2,1:T(8,128)(2,1)} %copy-done.3) | copy-start | bytes 1572868 | tf_op jit(solution)/shard_map/while
  91.6 2.9 %copy-start.8 = (bf16[1024,256]{0,1:T(8,128)(2,1)S(1)}, bf16[1024,256]{0,1:T(8,128)(2,1)}, u32[]{:S(2)}) copy-start(bf16[1024,256]{0,1:T(8,128)(2,1)} %copy-done.7) | copy-start | bytes 1572868 | tf_op jit(solution)/shard_map/while
  97.1 104.0 %reduce-scatter.5.cloned.1.call-start = ((), (), s32[]{:S(2)}) async-start(), calls=%async_computation.3 | async-start | bytes 589824 | tf_op jit(solution)/shard_map/reduce_scatter | solution.py:149
Sparse Core Ops, SparseCore 0:
  97.2 65.9 reduce-scatter.2
  166.9 34.1 reduce-scatter.4
